TPU v7x, 32 devices: a whole 2x2x4 slice. The times are simulated.
32 devices in a mesh: tile: 2 (over y), beam: 4 (over z), bl: 2 (over x), pol: 2 (over core).
Axes of the slice: x: 2, y: 2, z: 4, core: 2. Of those that a mesh axis runs over, the one named last changes fastest.
Arguments:
- sky_model: bfloat16 [4096, 4096], P(('tile', 'bl', 'pol'), 'beam'), parts along dimension 0, may hold values from -6 to 6
- beam_pattern: bfloat16 [8, 2048, 2048], P(('tile', 'beam'), ('bl', 'pol')), parts along dimension 0, may hold values from 0.099609375 to 1
- kernels: bfloat16 [8, 256, 128, 128], P(('tile', 'beam'), ('bl', 'pol')), parts along dimension 0, may hold values from -0.5 to 0.5
- observed: float32 [8, 256, 2, 128], P(('tile', 'beam'), ('bl', 'pol')), parts along dimension 0, may hold values from -6 to 6
- tile_owner: int32 [8, 256, 1], P(('tile', 'beam'), ('bl', 'pol')), parts along dimension 0, may hold values from 0 to 3; in each aligned block of 64 rows (0 to 63, 64 to 127, ..., all dimensions but the last counted through in order) at most 32 rows name the same one
- tile_local: int32 [8, 256], P(('tile', 'beam'), ('bl', 'pol')), parts along dimension 0, may hold values from 0 to 4095
- vis_count: int32 [8, 256], P(('tile', 'beam'), ('bl', 'pol')), parts along dimension 0, may hold values from 1 to 128
Outputs:
- residual_vis: float32 [8, 256, 2, 128], P(('tile', 'beam'), ('bl', 'pol')), parts along dimension 0
- dirty_grid: float32 [8, 16384, 2, 128], P(('tile', 'beam'), ('bl', 'pol')), parts along dimension 0
There are 2 independent parts, one for each index of `tile`. A program takes and returns all parts, laid end to end along the dimension named above; each array names one. Nothing has to cross between parts.
Inputs may be any that keep to these rules, and one draw needn't show every extreme that they name: `tile_owner`: among the 64 visibility tiles of one device, at most 32 name the same owner, and in some blocks one owner is named exactly 32 times.
All inputs are finite; a program needn't handle non-finite values.
Results may differ from a plain program's by a relative error of at most 0.0055.
Values may be sent and summed in bfloat16 or wider, within the bound.
A program may use at most 64 MiB of HBM per device.

v0:
```python
import math

import jax
import jax.numpy as jnp
from jax import lax
from jax.sharding import PartitionSpec as P

GRID = 2048
HALO = 512


def extended(block, sides, width):
    for axis, dim in sides:
        count = lax.axis_size(axis)
        forward = [(i, i + 1) for i in range(count - 1)]
        backward = [(target, source) for source, target in forward]
        low = lax.ppermute(
            lax.slice_in_dim(block, block.shape[dim] - width, None, axis=dim), axis, forward
        )
        high = lax.ppermute(lax.slice_in_dim(block, 0, width, axis=dim), axis, backward)
        block = jnp.concatenate([low, block, high], axis=dim)
    return block


def tables(rows, cols):
    row_index = jnp.arange(rows, dtype=jnp.int32)[:, None]
    col_index = jnp.arange(cols, dtype=jnp.int32)[None, :]
    angles = (row_index * col_index % GRID).astype(jnp.float32) * jnp.float32(2.0 * math.pi / GRID)
    factor = jnp.float32(1.0 / math.sqrt(GRID))
    return (
        (jnp.cos(angles) * factor).astype(jnp.bfloat16),
        (jnp.sin(angles) * factor).astype(jnp.bfloat16),
    )


def transform(table, image):
    return jnp.einsum("kux,yx->kuy", table, image, preferred_element_type=jnp.float32)


def weighted(pattern, values):
    return (pattern * values.astype(jnp.float32)).astype(jnp.bfloat16)


def on_device(sky_model, beam_pattern, kernels, observed, tile_owner, tile_local, vis_count):
    group = lax.axis_size(("bl", "pol"))
    cos_one, sin_one = tables(GRID // 2, GRID)
    first_table = jnp.stack([cos_one, -sin_one])
    pattern = beam_pattern[0].astype(jnp.float32)
    padded = extended(sky_model, (("beam", 1),), HALO)
    half_sum = transform(first_table, weighted(pattern, padded))
    half_plane = half_sum.astype(jnp.bfloat16)
    columns = lax.all_to_all(half_plane, ("bl", "pol"), split_axis=1, concat_axis=2, tiled=True)
    cos_two, sin_two = tables(GRID, GRID)
    real_part = columns[0]
    imag_part = columns[1]
    uv_real = jnp.dot(real_part, cos_two, preferred_element_type=jnp.float32) + jnp.dot(
        imag_part, sin_two, preferred_element_type=jnp.float32
    )
    uv_imag = jnp.dot(imag_part, cos_two, preferred_element_type=jnp.float32) - jnp.dot(
        real_part, sin_two, preferred_element_type=jnp.float32
    )
    uv_grid = jnp.stack([uv_real, uv_imag]).astype(jnp.bfloat16)
    u_rows = uv_grid.shape[1]
    cells = kernels.shape[3]
    grid_tiles = (
        uv_grid.reshape(2, u_rows // 8, 8, GRID // 16, 16)
        .transpose(1, 3, 0, 2, 4)
        .reshape(-1, 2, cells)
    )
    tiles_dev = grid_tiles.shape[0]
    owners = tile_owner[0, :, 0]
    local_ids = tile_local[0]
    vis_tiles = owners.shape[0]
    capacity = max(2, 2 * vis_tiles // group)
    onehot_owner = (owners[:, None] == jnp.arange(group, dtype=jnp.int32)[None, :]).astype(
        jnp.int32
    )
    ranking = jnp.cumsum(onehot_owner, axis=0) - onehot_owner
    slots = jnp.sum(ranking * onehot_owner, axis=1)
    destination = owners * capacity + slots
    request_ids = (
        jnp.full((group * capacity,), -1, jnp.int32)
        .at[destination]
        .set(local_ids)
        .reshape(group, capacity)
    )
    picked = grid_tiles[
        jnp.clip(
            lax.all_to_all(request_ids, ("bl", "pol"), split_axis=0, concat_axis=0, tiled=True),
            0,
            tiles_dev - 1,
        )
    ]
    returned = lax.all_to_all(picked, ("bl", "pol"), split_axis=0, concat_axis=0, tiled=True)
    fetched = returned.reshape(group * capacity, 2, cells)[destination]
    kernel_set = kernels[0]
    predicted = jnp.einsum("rjm,rcm->rcj", kernel_set, fetched, preferred_element_type=jnp.float32)
    live_mask = jnp.arange(cells, dtype=jnp.int32)[None, :] < vis_count[0][:, None]
    residual = jnp.where(live_mask[:, None, :], observed[0] - predicted, jnp.zeros_like(predicted))
    residual_low = residual.astype(jnp.bfloat16)
    contribution = jnp.einsum(
        "rjm,rcj->rcm", kernel_set, residual_low, preferred_element_type=jnp.float32
    )
    send_terms = (
        jnp.zeros((group * capacity, 2, cells), jnp.float32)
        .at[destination]
        .set(contribution)
        .reshape(group, capacity, 2, cells)
    )
    arrived, arrived_ids = (
        lax.all_to_all(
            send_terms.astype(jnp.bfloat16), ("bl", "pol"), split_axis=0, concat_axis=0, tiled=True
        ).astype(send_terms.dtype),
        lax.all_to_all(request_ids, ("bl", "pol"), split_axis=0, concat_axis=0, tiled=True),
    )
    flat_ids = arrived_ids.reshape(-1)
    valid = flat_ids >= 0
    terms = jnp.where(
        valid[:, None, None],
        arrived.reshape(-1, 2, cells),
        jnp.zeros((flat_ids.shape[0], 2, cells), jnp.float32),
    )
    dirty = (
        jnp.zeros((tiles_dev, 2, cells), jnp.float32)
        .at[jnp.clip(flat_ids, 0, tiles_dev - 1)]
        .add(terms)
    )
    return (residual[None], dirty[None])


def solution(mesh):
    placed = (
        P(("tile", "bl", "pol"), "beam"),
        P(("tile", "beam"), ("bl", "pol"), None),
        P(("tile", "beam"), ("bl", "pol"), None, None),
        P(("tile", "beam"), ("bl", "pol"), None, None),
        P(("tile", "beam"), ("bl", "pol"), None),
        P(("tile", "beam"), ("bl", "pol")),
        P(("tile", "beam"), ("bl", "pol")),
    )
    return jax.shard_map(
        on_device,
        mesh=mesh,
        in_specs=placed,
        out_specs=(
            P(("tile", "beam"), ("bl", "pol"), None, None),
            P(("tile", "beam"), ("bl", "pol"), None, None),
        ),
        check_vma=False,
    )
```

profile of v0, /device:TPU:0, one launch (start us, length us, event | category | flops | bytes accessed | tf_op | source)
XLA Modules:
  0.0 486.9 jit_solution(12809098943594819605)
XLA Ops:
  0.7 2.4 fusion.78
  3.0 5.8 %collective-permute-start = (bf16[512,512]{1,0:T(8,128)(2,1)}, bf16[512,512]{1,0:T(8,128)(2,1)}, u32[]{:S(2)}, u32[]{:S(2)}) collective-permute-start(bf16[512,512]{1,0:T(8,128)(2,1)} %get-tuple-element.4), channel_id=1, source_target_pairs={{0,4},{4,8},{8,12},{1,5},{5,9},{9,13},{2,6},{6,10},{10,14},{3,7},{... | collective-permute-start | bytes 1572872 | tf_op jit(solution)/shard_map/ppermute | solution.py:17
  14.0 3.2 all-to-all-start.1
  17.2 31.2 %fusion.20 = bf16[1,1024,2048]{2,1,0:T(8,128)(2,1)S(1)} fusion(), kind=kLoop, calls=%fused_computation.35 | loop fusion | flops 39845888 | bytes 4194304 | tf_op jit(solution)/shard_map/neg | solution.py:47
  48.5 31.0 %multiply_convert_fusion.7 = bf16[1,1024,2048]{2,1,0:T(8,128)(2,1)S(1)} fusion(), kind=kLoop, calls=%fused_computation.31 | loop fusion | flops 33554432 | bytes 4194304 | tf_op jit(solution)/shard_map/convert_element_type | solution.py:31
  79.5 5.9 %fusion.38 = bf16[2,1024,512]{2,1,0:T(8,128)(2,1)S(1)} fusion(bf16[512,512]{1,0:T(8,128)(2,1)} %collective-permute-done.1, bf16[512,1024]{1,0:T(8,128)(2,1)S(1)} %copy-done.1, bf16[512,512]{1,0:T(8,128)(2,1)} %collective-permute-done, bf16[1,512,2048]{2,1,0:T(8,128)(2,1)S(1)} %copy-done.6, bf16[1,1024,2048]{2,1,0:T(8,128)(2,1)S(1)} %fusion.20, ...), kind=kOutput, calls=%fused_computation.54 | convolution fusion | flops 4309647360 | bytes 14680064 | tf_op jit(solution)/shard_map/kux,yx->kuy/dot_general | solution.py:37
  85.4 3.5 copy.26
  88.9 4.4 all-to-all-start
  93.7 25.4 %all-to-all-done = bf16[2,1024,512]{2,0,1:T(2,128)(2,1)} async-done(((bf16[2,1024,512]{2,0,1:T(2,128)(2,1)}), bf16[2,1024,512]{2,0,1:T(2,128)(2,1)}, u32[]{:S(2)}, u32[]{:S(2)}) %all-to-all-start) | async-done | bytes 2097184 | tf_op jit(solution)/shard_map/all_to_all | solution.py:52
  119.1 1.9 copy.27
  122.2 2.3 copy.28
  124.5 75.1 %fusion.14 = f32[256,2048]{1,0:T(8,128)} fusion(bf16[256,2048]{0,1:T(8,128)(2,1)} %bitcast.70), kind=kOutput, calls=%fused_computation.27 | convolution fusion | flops 2214592512 | bytes 3145728 | tf_op jit(solution)/shard_map/dot_general | solution.py:56
  199.6 1.3 copy.29
  200.9 64.5 %fusion.13 = f32[256,2048]{1,0:T(8,128)} fusion(bf16[256,2048]{0,1:T(8,128)(2,1)} %bitcast.72), kind=kOutput, calls=%fused_computation.26 | convolution fusion | flops 2214592512 | bytes 3145728 | tf_op jit(solution)/shard_map/dot_general | solution.py:59
  265.5 64.7 %fusion.25 = bf16[256,2048]{1,0:T(8,128)(2,1)S(1)} fusion(f32[256,2048]{1,0:T(8,128)S(1)} %copy-done.7, bf16[256,2048]{0,1:T(8,128)(2,1)S(1)} %bitcast.73), kind=kOutput, calls=%fused_computation.41 | convolution fusion | flops 2215641088 | bytes 4194304 | tf_op jit(solution)/shard_map/dot_general | solution.py:56
  330.2 8.2 %stack.15 = bf16[1,32,8,128,16]{4,3,2,1,0:T(8,128)(2,1)} reshape(bf16[256,2048]{1,0:T(8,128)(2,1)S(1)} %fusion.25) | data formatting | bytes 2097152 | tf_op jit(solution)/shard_map/stack | solution.py:62
  338.4 7.1 %copy.30 = bf16[1,32,8,128,16]{3,4,2,1,0:T(8,128)(2,1)S(1)} copy(bf16[1,32,8,128,16]{4,3,2,1,0:T(8,128)(2,1)} %stack.15) | data formatting | bytes 2097152 | tf_op jit(solution)/shard_map/stack | solution.py:62
  345.5 67.0 %fusion.24 = bf16[256,2048]{1,0:T(8,128)(2,1)} fusion(f32[256,2048]{1,0:T(8,128)} %fusion.13, bf16[256,2048]{0,1:T(8,128)(2,1)} %bitcast.71), kind=kOutput, calls=%fused_computation.40 | convolution fusion | flops 2215641088 | bytes 4194304 | tf_op jit(solution)/shard_map/dot_general | solution.py:59
  412.5 9.1 %stack.16 = bf16[1,32,8,128,16]{4,3,2,1,0:T(8,128)(2,1)} reshape(bf16[256,2048]{1,0:T(8,128)(2,1)} %fusion.24) | data formatting | bytes 2097152 | tf_op jit(solution)/shard_map/stack | solution.py:62
  421.6 7.5 %copy.31 = bf16[1,32,8,128,16]{3,4,2,1,0:T(8,128)(2,1)} copy(bf16[1,32,8,128,16]{4,3,2,1,0:T(8,128)(2,1)} %stack.16) | data formatting | bytes 2097152 | tf_op jit(solution)/shard_map/stack | solution.py:62
  429.1 1.4 maximum_bitcast_fusion
  430.6 2.7 copy.32
  433.3 4.2 reshape.221
  437.4 6.2 %copy.34 = bf16[4096,2,128]{2,1,0:T(2,128)(2,1)} copy(bf16[4096,2,128]{0,2,1:T(8,128)(2,1)} %reshape.221) | data formatting | bytes 4194304 | tf_op jit(solution)/shard_map/reshape | solution.py:68
  443.6 2.3 gather_fusion
  446.5 3.5 all-to-all-start.2
  450.1 4.1 all-to-all-done.2
  456.8 2.4 scatter_fusion
  459.9 3.3 all-to-all-start.3
  463.3 4.0 all-to-all-done.3
  467.5 2.8 broadcast_in_dim.48
  470.3 16.2 %scatter_fusion.1 = f32[4096,2,128]{2,1,0:T(2,128)} fusion(f32[4096,2,128]{2,1,0:T(2,128)} %broadcast_in_dim.48, s32[128]{0:T(128)S(1)} %fusion.52, f32[128,2,128]{2,1,0:T(2,128)S(1)} %convert_select_fusion), kind=kCustom, calls=%fused_computation.4 | custom fusion | flops 32768 | bytes 393728 | tf_op jit(solution)/shard_map/scatter-add | solution.py:126
  (46 shorter events, 10.9 us)
Async XLA Ops:
  0.6 454.3 %copy-start = (bf16[1,64,128,128]{3,2,1,0:T(8,128)(2,1)S(1)}, bf16[1,64,128,128]{3,2,1,0:T(8,128)(2,1)}, u32[]{:S(2)}) copy-start(bf16[1,64,128,128]{3,2,1,0:T(8,128)(2,1)} %param.9) | copy-start | bytes 6291460
  0.6 78.8 %copy-start.1 = (bf16[512,1024]{1,0:T(8,128)(2,1)S(1)}, bf16[512,1024]{1,0:T(8,128)(2,1)}, u32[]{:S(2)}) copy-start(bf16[512,1024]{1,0:T(8,128)(2,1)} %param.7) | copy-start | bytes 3145732
  3.0 76.4 %collective-permute-start = (bf16[512,512]{1,0:T(8,128)(2,1)}, bf16[512,512]{1,0:T(8,128)(2,1)}, u32[]{:S(2)}, u32[]{:S(2)}) collective-permute-start(bf16[512,512]{1,0:T(8,128)(2,1)} %get-tuple-element.4), channel_id=1, source_target_pairs={{0,4},{4,8},{8,12},{1,5},{5,9},{9,13},{2,6},{6,10},{10,14},{3,7},{... | collective-permute-start | bytes 1572872 | tf_op jit(solution)/shard_map/ppermute | solution.py:17
  8.8 70.7 %collective-permute-start.1 = (bf16[512,512]{1,0:T(8,128)(2,1)}, bf16[512,512]{1,0:T(8,128)(2,1)}, u32[]{:S(2)}, u32[]{:S(2)}) collective-permute-start(bf16[512,512]{1,0:T(8,128)(2,1)} %get-tuple-element.5), channel_id=1, source_target_pairs={{4,0},{8,4},{12,8},{5,1},{9,5},{13,9},{6,2},{10,6},{14,10},{7,3},{... | collective-permute-start | bytes 1572872 | tf_op jit(solution)/shard_map/ppermute | solution.py:20
  14.0 74.9 %all-to-all-start.1 = ((s32[4,1,32]{2,1,0:T(1,128)}), s32[4,1,32]{2,1,0:T(1,128)S(1)}, u32[]{:S(2)}, u32[]{:S(2)}) async-start(s32[4,1,32]{2,1,0:T(1,128)} %bitcast.15), calls=%async_computation.1 | async-start | bytes 4096 | tf_op jit(solution)/shard_map/all_to_all | solution.py:89
  17.2 62.3 %copy-start.6 = (bf16[1,512,2048]{2,1,0:T(8,128)(2,1)S(1)}, bf16[1,512,2048]{2,1,0:T(8,128)(2,1)}, u32[]{:S(2)}) copy-start(bf16[1,512,2048]{2,1,0:T(8,128)(2,1)} %param.8) | copy-start | bytes 6291460
  85.4 8.0 %copy-start.5 = (s32[1,64]{1,0:T(1,128)S(1)}, s32[1,64]{1,0:T(1,128)}, u32[]{:S(2)}) copy-start(s32[1,64]{1,0:T(1,128)} %param.13) | copy-start | bytes 772
  88.9 30.2 %all-to-all-start = ((bf16[2,1024,512]{2,0,1:T(2,128)(2,1)}), bf16[2,1024,512]{2,0,1:T(2,128)(2,1)}, u32[]{:S(2)}, u32[]{:S(2)}) async-start(bf16[2,1024,512]{2,0,1:T(2,128)(2,1)} %copy.26), calls=%async_computation | async-start | bytes 4194304 | tf_op jit(solution)/shard_map/all_to_all | solution.py:52
  200.9 64.6 %copy-start.2 = (bf16[1,256,4,512]{1,3,2,0:T(8,128)(2,1)S(1)}, bf16[1,256,4,512]{1,3,2,0:T(8,128)(2,1)}, u32[]{:S(2)}) copy-start(bf16[1,256,4,512]{1,3,2,0:T(8,128)(2,1)} %copy.29) | copy-start | bytes 3145732
  200.9 64.6 %copy-start.7 = (f32[256,2048]{1,0:T(8,128)S(1)}, f32[256,2048]{1,0:T(8,128)}, u32[]{:S(2)}) copy-start(f32[256,2048]{1,0:T(8,128)} %fusion.14) | copy-start | bytes 6291460
  429.1 25.8 %copy-start.4 = (f32[1,64,2,128]{3,2,1,0:T(2,128)S(1)}, f32[1,64,2,128]{3,2,1,0:T(2,128)}, u32[]{:S(2)}) copy-start(f32[1,64,2,128]{3,2,1,0:T(2,128)} %param.10) | copy-start | bytes 196612
  446.5 7.6 %all-to-all-start.2 = ((bf16[4,32,2,128]{3,1,2,0:T(8,128)(2,1)}), bf16[4,32,2,128]{3,1,2,0:T(8,128)(2,1)S(1)}, u32[]{:S(2)}, u32[]{:S(2)}) async-start(bf16[4,32,2,128]{3,1,2,0:T(8,128)(2,1)} %copy.36), calls=%async_computation.2 | async-start | bytes 131072 | tf_op jit(solution)/shard_map/all_to_all | solution.py:94
  456.1 30.4 %copy-start.3 = (f32[64,2,128]{2,1,0:T(2,128)}, f32[64,2,128]{2,1,0:T(2,128)S(1)}, u32[]{:S(2)}) copy-start(f32[64,2,128]{2,1,0:T(2,128)S(1)} %fusion.46) | copy-start | bytes 196612
  459.9 7.4 %all-to-all-start.3 = ((bf16[4,32,2,128]{3,2,1,0:T(2,128)(2,1)}), bf16[4,32,2,128]{3,2,1,0:T(2,128)(2,1)S(1)}, u32[]{:S(2)}, u32[]{:S(2)}) async-start(bf16[4,32,2,128]{3,2,1,0:T(2,128)(2,1)} %bitcast.22), calls=%async_computation.3 | async-start | bytes 131072 | tf_op jit(solution)/shard_map/all_to_all | solution.py:111
where the time goes:
time: 496 us; the launch traced here: 487 us
  matrix products  279 us (56%)
  other arithmetic  83.2 us (17%)
  local copies, waits for them, and re-layouts  68.3 us (14%)
  waiting for transfers between devices  33.5 us (7%)
  starting transfers between devices  21.5 us (4%)
    dot_general x1, matrix products, on_device(): jnp.dot(real_part, cos_two, preferred_element_type=jnp.float32)  75.1 us
    dot_general x1, matrix products, on_device(): jnp.dot(real_part, sin_two, preferred_element_type=jnp.float32)  67 us
    dot_general x1, matrix products, on_device(): jnp.dot(imag_part, sin_two, preferred_element_type=jnp.float32)  64.7 us
    dot_general x1, matrix products, on_device(): jnp.dot(imag_part, cos_two, preferred_element_type=jnp.float32)  64.5 us
    another operation x4, local copies, waits for them, and re-layouts, on_device(): uv_grid = jnp.stack([uv_real, uv_imag]).astype(jnp.bfloat16)  31.9 us
    neg x1, other arithmetic, on_device(): first_table = jnp.stack([cos_one, -sin_one])  31.2 us
    convert_element_type x1, other arithmetic, tables(): (jnp.cos(angles) * factor).astype(jnp.bfloat16)  31 us
    all_to_all x1, waiting for transfers between devices, on_device(): lax.all_to_all(half_plane, ('bl', 'pol'), split_axis=1, concat_axis=2, ti...  25.4 us
  transfers between devices with their start and end apart: 6, of which 3 were waited for; matrix products, arithmetic and copies ran while one was open for 15% of the time, Pallas kernels for 0%

commit v1 on v0

v1 whole, which is shorter than its diff:
```python
import functools
import math

import jax
import jax.numpy as jnp
import numpy as np
from jax import lax
from jax.experimental import pallas as pl
from jax.experimental.pallas import tpu as pltpu
from jax.sharding import PartitionSpec as P

MESH = pl.DeviceIdType.MESH
RADIX = 8
WIDE = 16
VMEM = pl.BlockSpec(memory_space=pltpu.VMEM)
SMEM = pl.BlockSpec(memory_space=pltpu.SMEM)
ANY = pl.BlockSpec(memory_space=pl.ANY)
NT = (((1,), (1,)), ((), ()))
NN = (((1,), (0,)), ((), ()))


def wave(rows, cols, period, factor):
    angle = (np.outer(rows, cols) % period) * (2.0 * math.pi / period)
    return np.cos(angle) * factor, np.sin(angle) * factor


def first_tables(grid):
    span = grid // RADIX
    blocks = grid // 2 // RADIX
    cols = np.arange(span)

    def of(i):
        return wave(RADIX * np.arange(blocks) + i, cols, grid, grid**-0.5)

    real = []
    for i in (0, RADIX // 2):
        cos, sin = of(i)
        real.append(np.concatenate([cos, -sin], 0))
    pairs = []
    for i in range(1, RADIX // 2):
        cos, sin = of(i)
        cos_m, sin_m = of(RADIX - i)
        pairs.append(
            np.concatenate(
                [
                    np.concatenate([cos, sin], 1),
                    np.concatenate([-sin, cos], 1),
                    np.concatenate([cos_m, -sin_m], 1),
                    np.concatenate([-sin_m, -cos_m], 1),
                ],
                0,
            )
        )
    return np.stack(real).astype(jnp.bfloat16), np.stack(pairs).astype(jnp.bfloat16)


def second_tables(grid, rows):
    period = grid // WIDE
    phase = np.stack(wave(np.arange(period), np.arange(period), period, 1.0)).astype(np.float32)
    cos, sin = wave(np.arange(grid), np.arange(WIDE), grid, grid**-0.5)
    cos, sin = np.tile(cos, (1, RADIX)), np.tile(sin, (1, RADIX))
    cos, sin = cos.reshape(-1, rows, cos.shape[1]), sin.reshape(-1, rows, sin.shape[1])
    table = np.concatenate([np.concatenate([cos, -sin], 2), np.concatenate([sin, cos], 2)], 1)
    return phase, table.astype(jnp.bfloat16)


def group_index():
    return lax.axis_index("bl") * lax.axis_size("pol") + lax.axis_index("pol")


def group_device(index):
    pol = lax.axis_size("pol")
    return {"bl": lax.div(index, pol), "pol": lax.rem(index, pol)}


def halo_kernel(group, beams, sky, code, low, high, codes, send, recv, local):
    beam = lax.axis_index("beam")
    me = group_index()
    barrier = pltpu.get_barrier_semaphore()
    width = low.shape[1]
    to_next = pltpu.make_async_remote_copy(
        src_ref=sky.at[:, pl.ds(sky.shape[1] - width, width)], dst_ref=low,
        send_sem=send.at[0], recv_sem=recv.at[0],
        device_id={"beam": beam + 1}, device_id_type=MESH,
    )
    to_last = pltpu.make_async_remote_copy(
        src_ref=sky.at[:, pl.ds(0, width)], dst_ref=high,
        send_sem=send.at[1], recv_sem=recv.at[1],
        device_id={"beam": beam - 1}, device_id_type=MESH,
    )
    has_next, has_last = beam < beams - 1, beam > 0
    for step in range(1, group):
        pl.semaphore_signal(barrier, inc=1, device_id=group_device(lax.rem(me + step, group)), device_id_type=MESH)

    @pl.when(has_next)
    def _():
        pl.semaphore_signal(barrier, inc=1, device_id={"beam": beam + 1}, device_id_type=MESH)

    @pl.when(has_last)
    def _():
        pl.semaphore_signal(barrier, inc=1, device_id={"beam": beam - 1}, device_id_type=MESH)

    edges = jnp.where(beam < beams - 1, 1, 0) + jnp.where(beam > 0, 1, 0)
    pl.semaphore_wait(barrier, group - 1 + edges)

    @pl.when(has_next)
    def _():
        to_next.start()

    @pl.when(has_last)
    def _():
        to_last.start()

    copies = []
    for step in range(1, group):
        copy = pltpu.make_async_remote_copy(
            src_ref=code, dst_ref=codes.at[me],
            send_sem=send.at[1 + step], recv_sem=recv.at[1 + step],
            device_id=group_device(lax.rem(me + step, group)), device_id_type=MESH,
        )
        copy.start()
        copies.append(copy)
    own = pltpu.make_async_copy(code, codes.at[me], local)
    own.start()
    own.wait()
    for copy in copies:
        copy.wait()

    @pl.when(has_next)
    def _():
        to_next.wait_send()

    @pl.when(has_last)
    def _():
        to_last.wait_send()

    @pl.when(has_last)
    def _():
        to_next.wait_recv()

    @pl.when(has_next)
    def _():
        to_last.wait_recv()


def transform_rows(beams, image, half, pattern, sky, low, high, real_table, pair_table, g_real, g_pair, re, im):
    rows = pattern.shape[0]
    span = pattern.shape[1] // RADIX
    width = low.shape[1]
    beam = lax.axis_index("beam")
    step = 32
    root = math.sqrt(0.5)

    def fold(index, carry):
        at = pl.ds(pl.multiple_of(index * step, step), step)
        left = jnp.where(beam > 0, low[at, :], jnp.zeros((step, width), low.dtype))
        right = jnp.where(beam < beams - 1, high[at, :], jnp.zeros((step, width), high.dtype))
        window = jnp.concatenate([left, sky[at, :], right], axis=1)
        parts = []
        for a in range(RADIX):
            cut = slice(a * span, (a + 1) * span)
            weighted = pattern[at, cut].astype(jnp.float32) * window[:, cut].astype(jnp.float32)
            parts.append(weighted.astype(jnp.bfloat16).astype(jnp.float32))
        s = [parts[a] + parts[a + 4] for a in range(4)]
        d = [parts[a] - parts[a + 4] for a in range(4)]
        even, odd = s[0] + s[2], s[1] + s[3]
        near, far = root * (d[1] - d[3]), root * (d[1] + d[3])

        def put(ref, lead, off, value):
            ref[lead, at, off : off + span] = value.astype(jnp.bfloat16)

        put(g_real, 0, 0, even + odd)
        put(g_real, 1, 0, even - odd)
        put(g_pair, 0, 0, d[0] + near)
        put(g_pair, 0, span, -(d[2] + far))
        put(g_pair, 1, 0, s[0] - s[2])
        put(g_pair, 1, span, s[3] - s[1])
        put(g_pair, 2, 0, d[0] - near)
        put(g_pair, 2, span, d[2] - far)
        return carry

    lax.fori_loop(0, rows // step, fold, 0)
    blocks = re.shape[1] // RADIX
    lanes = re.shape[2]

    def place(ref, i, value):
        for k in range(ref.shape[0]):
            ref[k, pl.ds(i, blocks, stride=RADIX), :] = value[:, k * lanes : (k + 1) * lanes]

    for k, i in enumerate((0, RADIX // 2)):
        out = lax.dot_general(real_table[k], g_real[k], NT, preferred_element_type=jnp.float32)
        place(re, i, out[:blocks])
        place(im, i, out[blocks:])
    for k in range(RADIX // 2 - 1):
        out = lax.dot_general(pair_table[k], g_pair[k], NT, preferred_element_type=jnp.float32)
        for n, (ref, i) in enumerate(((re, k + 1), (im, k + 1), (re, RADIX - 1 - k), (im, RADIX - 1 - k))):
            place(ref, i, out[n * blocks : (n + 1) * blocks])


def asked_tiles(codes, phase, table, re, im, turned, part):
    group, _, lanes = codes.shape
    period = phase.shape[1]
    vis = part.shape[0] // group
    cells = RADIX * WIDE
    own = lax.broadcasted_iota(jnp.int32, (RADIX, 2 * cells), 0)
    column = lax.broadcasted_iota(jnp.int32, (RADIX, 2 * cells), 1)
    keep = own == (column % cells) // WIDE
    weights = table[group_index()]

    def one(asker, r):
        tile = codes[asker, 0, r]
        up = tile // period
        at = pl.ds(pl.multiple_of(up * RADIX, RADIX), RADIX)
        turn = tile - up * period
        cos = phase[0, pl.ds(turn, 1), :]
        sin = phase[1, pl.ds(turn, 1), :]
        real, imag = [], []
        for k in range(re.shape[0]):
            x, y = re[k, at, :], im[k, at, :]
            real.append(x * cos + y * sin)
            imag.append(y * cos - x * sin)
        return jnp.concatenate(real + imag, axis=1)

    def of_asker(asker, carry):
        def turn_pair(p, inner):
            both = jnp.concatenate([one(asker, 2 * p), one(asker, 2 * p + 1)], axis=0)
            turned[pl.ds(pl.multiple_of(p * 2 * RADIX, 2 * RADIX), 2 * RADIX), :] = both.astype(jnp.bfloat16)
            return inner

        lax.fori_loop(0, vis // 2, turn_pair, 0, unroll=4)
        cells_of = lax.dot_general(turned[...], weights, NN, preferred_element_type=jnp.float32)
        picked = jnp.where(keep[None], cells_of.reshape(vis, RADIX, 2 * cells), 0.0)
        part[pl.ds(pl.multiple_of(asker * vis, vis), vis), :] = jnp.sum(picked, axis=1).astype(part.dtype)
        return carry

    lax.fori_loop(0, group, of_asker, 0)


def tiles_kernel(
    beams, pattern, sky, low, high, codes, real_table, pair_table, phase, table, part,
    g_real, g_pair, re, im, turned,
):
    transform_rows(beams, None, None, pattern, sky, low, high, real_table, pair_table, g_real, g_pair, re, im)
    asked_tiles(codes, phase, table, re, im, turned, part)


def exchange(group, source_of, target, send, recv):
    me = group_index()
    copies = []
    for step in range(1, group):
        peer = lax.rem(me + step, group)
        copy = pltpu.make_async_remote_copy(
            src_ref=source_of(peer), dst_ref=target.at[me],
            send_sem=send.at[step - 1], recv_sem=recv.at[step - 1],
            device_id=group_device(peer), device_id_type=MESH,
        )
        copy.start()
        copies.append(copy)
    return copies


def residual_kernel(
    group, part, kernels, observed, counts, residual, shared,
    came, given, wide, narrow, send, recv, send_two, recv_two,
):
    me = group_index()
    vis = given.shape[0]
    cells = kernels.shape[1]
    barrier = pltpu.get_barrier_semaphore()
    for step in range(1, group):
        pl.semaphore_signal(barrier, inc=1, device_id=group_device(lax.rem(me + step, group)), device_id_type=MESH)
    pl.semaphore_wait(barrier, group - 1)
    first = exchange(group, lambda peer: part.at[pl.ds(pl.multiple_of(peer * vis, vis), vis)], came, send, recv)
    mine = part[pl.ds(pl.multiple_of(me * vis, vis), vis), :].astype(jnp.float32)
    wide[...] = jnp.zeros_like(wide)
    live = lax.broadcasted_iota(jnp.int32, (vis, vis), 0) == lax.broadcasted_iota(jnp.int32, (vis, vis), 1)
    count = jnp.sum(jnp.where(live, counts[...].astype(jnp.float32), 0.0), axis=1, keepdims=True)
    mask = lax.broadcasted_iota(jnp.int32, (vis, cells), 1).astype(jnp.float32) < count
    for copy in first:
        copy.wait()
    for step in range(1, group):
        mine = mine + came[lax.rem(me + step, group)].astype(jnp.float32)
    for c in range(2):
        wide[pl.ds(c, vis, stride=RADIX), :] = mine[:, c * cells : (c + 1) * cells]

    def predict(r, carry):
        at = pl.ds(pl.multiple_of(r * RADIX, RADIX), RADIX)
        narrow[at, :] = lax.dot_general(
            wide[at, :].astype(jnp.bfloat16), kernels[r], NT, preferred_element_type=jnp.float32
        )
        return carry

    lax.fori_loop(0, vis, predict, 0, unroll=8)
    for c in range(2):
        seen = observed[pl.ds(c, vis, stride=2), :]
        left = jnp.where(mask, seen - narrow[pl.ds(c, vis, stride=RADIX), :], 0.0)
        residual[pl.ds(c, vis, stride=2), :] = left
        wide[pl.ds(c, vis, stride=RADIX), :] = left

    def grid_back(r, carry):
        at = pl.ds(pl.multiple_of(r * RADIX, RADIX), RADIX)
        narrow[at, :] = lax.dot_general(
            wide[at, :].astype(jnp.bfloat16), kernels[r], NN, preferred_element_type=jnp.float32
        )
        return carry

    lax.fori_loop(0, vis, grid_back, 0, unroll=8)
    for c in range(2):
        given[:, c * cells : (c + 1) * cells] = narrow[pl.ds(c, vis, stride=RADIX), :].astype(given.dtype)
    second = exchange(group, lambda peer: given, shared, send_two, recv_two)
    shared[me] = given[...]
    for copy in second:
        copy.wait()


def dirty_kernel(keys, terms, dirty):
    rows = dirty.shape[0] // 2
    cells = dirty.shape[1]
    step = 256
    start = pl.program_id(0) * rows
    key = keys[...]

    def some(index, carry):
        tile = lax.broadcasted_iota(jnp.int32, (step, key.shape[1]), 0) + (start + index * step)
        onehot = jnp.where(tile == key, 1.0, 0.0).astype(jnp.bfloat16)
        out = lax.dot_general(onehot, terms[...], NN, preferred_element_type=jnp.float32)
        for c in range(2):
            dirty[pl.ds(index * step * 2 + c, step, stride=2), :] = out[:, c * cells : (c + 1) * cells]
        return carry

    lax.fori_loop(0, rows // step, some, 0)


def on_device(sky_model, beam_pattern, kernels, observed, tile_owner, tile_local, vis_count):
    group = lax.axis_size(("bl", "pol"))
    beams = lax.axis_size("beam")
    rows, grid = beam_pattern.shape[1:]
    strip = sky_model.shape[1]
    halo = (grid - strip) // 2
    vis, cells = kernels.shape[1], kernels.shape[3]
    tiles_all = (grid // 2 // RADIX) * (grid // WIDE)
    tiles_dev = tiles_all // group
    lanes = 128
    code = tile_owner[0, :, 0] * tiles_dev + tile_local[0]
    code = jnp.broadcast_to(jnp.pad(code, (0, lanes - vis))[None], (8, lanes))
    f32, bf16 = jnp.float32, jnp.bfloat16

    low, high, codes = pl.pallas_call(
        functools.partial(halo_kernel, group, beams),
        out_shape=(
            jax.ShapeDtypeStruct((rows, halo), bf16),
            jax.ShapeDtypeStruct((rows, halo), bf16),
            jax.ShapeDtypeStruct((group, 8, lanes), jnp.int32),
        ),
        in_specs=[ANY, ANY],
        out_specs=(ANY, ANY, ANY),
        scratch_shapes=[
            pltpu.SemaphoreType.DMA((group + 1,)),
            pltpu.SemaphoreType.DMA((group + 1,)),
            pltpu.SemaphoreType.DMA(()),
        ],
        compiler_params=pltpu.CompilerParams(collective_id=0, has_side_effects=True),
        name="halo",
    )(sky_model, code)

    real_table, pair_table = first_tables(grid)
    phase, table = second_tables(grid, rows)
    span, period = grid // RADIX, grid // WIDE
    part = pl.pallas_call(
        functools.partial(tiles_kernel, beams),
        out_shape=jax.ShapeDtypeStruct((group * vis, 2 * cells), bf16),
        in_specs=[VMEM, VMEM, VMEM, VMEM, SMEM, VMEM, VMEM, VMEM, VMEM],
        out_specs=VMEM,
        scratch_shapes=[
            pltpu.VMEM((2, rows, span), bf16),
            pltpu.VMEM((RADIX // 2 - 1, rows, 2 * span), bf16),
            pltpu.VMEM((rows // period, grid // 2, period), f32),
            pltpu.VMEM((rows // period, grid // 2, period), f32),
            pltpu.VMEM((vis * RADIX, 2 * rows), bf16),
        ],
        compiler_params=pltpu.CompilerParams(vmem_limit_bytes=48 * 1024 * 1024),
        name="tiles",
    )(
        beam_pattern[0], sky_model, low, high, codes,
        jnp.asarray(real_table), jnp.asarray(pair_table), jnp.asarray(phase), jnp.asarray(table),
    )

    residual, shared = pl.pallas_call(
        functools.partial(residual_kernel, group),
        out_shape=(
            jax.ShapeDtypeStruct((vis * 2, cells), f32),
            jax.ShapeDtypeStruct((group, vis, 2 * cells), bf16),
        ),
        in_specs=[VMEM] * 4,
        out_specs=(VMEM, VMEM),
        scratch_shapes=[
            pltpu.VMEM((group, vis, 2 * cells), bf16),
            pltpu.VMEM((vis, 2 * cells), bf16),
            pltpu.VMEM((vis * RADIX, cells), f32),
            pltpu.VMEM((vis * RADIX, cells), f32),
            pltpu.SemaphoreType.DMA((group - 1,)),
            pltpu.SemaphoreType.DMA((group - 1,)),
            pltpu.SemaphoreType.DMA((group - 1,)),
            pltpu.SemaphoreType.DMA((group - 1,)),
        ],
        compiler_params=pltpu.CompilerParams(collective_id=1, has_side_effects=True),
        name="residual",
    )(part, kernels[0], observed.reshape(vis * 2, cells), vis_count)

    keys = codes[:, 0, :vis].reshape(1, group * vis) - group_index() * tiles_dev
    blocks = 4
    dirty = pl.pallas_call(
        dirty_kernel,
        grid=(blocks,),
        out_shape=jax.ShapeDtypeStruct((tiles_dev * 2, cells), f32),
        in_specs=[
            pl.BlockSpec((1, group * vis), lambda i: (0, 0)),
            pl.BlockSpec((group * vis, 2 * cells), lambda i: (0, 0)),
        ],
        out_specs=pl.BlockSpec((tiles_dev * 2 // blocks, cells), lambda i: (i, 0)),
        name="dirty",
    )(keys, shared.reshape(group * vis, 2 * cells))
    return (
        residual.reshape(1, vis, 2, cells),
        dirty.reshape(1, tiles_dev, 2, cells),
    )


def solution(mesh):
    placed = (
        P(("tile", "bl", "pol"), "beam"),
        P(("tile", "beam"), ("bl", "pol"), None),
        P(("tile", "beam"), ("bl", "pol"), None, None),
        P(("tile", "beam"), ("bl", "pol"), None, None),
        P(("tile", "beam"), ("bl", "pol"), None),
        P(("tile", "beam"), ("bl", "pol")),
        P(("tile", "beam"), ("bl", "pol")),
    )
    return jax.shard_map(
        on_device,
        mesh=mesh,
        in_specs=placed,
        out_specs=(
            P(("tile", "beam"), ("bl", "pol"), None, None),
            P(("tile", "beam"), ("bl", "pol"), None, None),
        ),
        check_vma=False,
    )
```

time: 496 us -> 57.1 us (0.12); the launches traced: 487 us -> 56.6 us
  matrix products: 279 us -> 0 us
  other arithmetic: 83.2 us -> 0.7 us
  local copies, waits for them, and re-layouts: 68.3 us -> 9.81 us
  Pallas kernels: 0 us -> 45.4 us
  waiting for transfers between devices: 33.5 us -> 0 us
  starting transfers between devices: 21.5 us -> 0 us
    dot_general x7 -> x0, matrix products: 279 us -> none  [the longest x1 75.1 us: on_device(): jnp.dot(real_part, cos_two, preferred_element_type=jnp.float32)]
    pallas_call x0 -> x4, Pallas kernels: none -> 45.4 us  [the longest x1 17.2 us: on_device(): pl.pallas_call(functools.partial(halo_kernel, group, beams), out_shape=(j...]
    all_to_all x4 -> x0, waiting for transfers between devices: 33.5 us -> none  [the longest x1 25.4 us: on_device(): lax.all_to_all(half_plane, ('bl', 'pol'), split_axis=1, concat_axis=2, ti...]
    convert_element_type x3 -> x0, other arithmetic: 32.4 us -> none  [the longest x1 31 us: tables(): (jnp.cos(angles) * factor).astype(jnp.bfloat16)]
    another operation x5 -> x0, local copies, waits for them, and re-layouts: 32 us -> none  [the longest x4 31.9 us: on_device(): uv_grid = jnp.stack([uv_real, uv_imag]).astype(jnp.bfloat16)]
    neg x1 -> x0, other arithmetic: 31.2 us -> none  [on_device(): first_table = jnp.stack([cos_one, -sin_one])]
    scatter-add x1 -> x0, other arithmetic: 16.2 us -> none  [on_device(): dirty = jnp.zeros((tiles_dev, 2, cells), jnp.float32).at[jnp.clip(flat_id...]
    all_to_all x4 -> x0, starting transfers between devices: 14.5 us -> none  [the longest x1 4.45 us: on_device(): lax.all_to_all(half_plane, ('bl', 'pol'), split_axis=1, concat_axis=2, ti...]
  transfers between devices with their start and end apart: 6 -> 0, of which waited for: 3 -> 0; matrix products, arithmetic and copies ran while one was open for 15% -> 0% of each run, Pallas kernels for 0% -> 0%
where the time goes in v1:
time: 57.1 us; the launch traced here: 56.6 us
  Pallas kernels  45.4 us (80%)
  local copies, waits for them, and re-layouts  9.81 us (17%)
  other arithmetic  0.7 us (1%)
  between operations  0.7 us (1%)
    pallas_call x1, Pallas kernels, on_device(): pl.pallas_call(functools.partial(halo_kernel, group, beams), out_shape=(j...  17.2 us
    pallas_call x1, Pallas kernels, on_device(): pl.pallas_call(functools.partial(residual_kernel, group), out_shape=(jax....  13.1 us
    pallas_call x1, Pallas kernels, on_device(): pl.pallas_call(functools.partial(tiles_kernel, beams), out_shape=jax.Shap...  10.1 us
    unnamed x19, local copies, waits for them, and re-layouts  8.56 us
    pallas_call x1, Pallas kernels, on_device(): pl.pallas_call(dirty_kernel, grid=(blocks,), out_shape=jax.ShapeDtypeStru...  5.15 us

profile of v1, /device:TPU:0, one launch (start us, length us, event | category | flops | bytes accessed | tf_op | source)
XLA Modules:
  0.0 56.6 jit_solution(7839670596523280977)
XLA Ops:
  0.6 0.7 %bitcast_add_fusion = s32[64]{0:T(128)S(1)} fusion(s32[1,64]{1,0:T(1,128)} %param.16, s32[1,64,1]{1,2,0:T(1,128)} %param.15), kind=kLoop, calls=%fused_computation.1 | loop fusion | flops 128 | bytes 768 | tf_op jit(solution)/shard_map/add | solution.py:344
  1.3 0.6 %broadcast_in_dim.2.code = s32[8,128]{1,0:T(8,128)} broadcast(s32[128]{0:T(128)S(1)} %pad.4), dimensions={1} | broadcast | bytes 4608 | tf_op jit(solution)/shard_map/broadcast_in_dim | solution.py:345
  1.9 17.2 %halo.1 = (bf16[512,512]{1,0:T(8,128)(2,1)}, bf16[512,512]{1,0:T(8,128)(2,1)}, s32[4,8,128]{2,1,0:T(8,128)}) custom-call(bf16[512,1024]{1,0:T(8,128)(2,1)} %sky.3, s32[8,128]{1,0:T(8,128)} %broadcast_in_dim.2.code), custom_call_target="tpu_custom_call" | custom-call | tf_op jit(solution)/shard_map/halo/pallas_call | solution.py:348
  19.1 0.0 copy-start
  19.1 1.2 %copy-done = bf16[512,1024]{1,0:T(8,128)(2,1)S(1)} copy-done((bf16[512,1024]{1,0:T(8,128)(2,1)S(1)}, bf16[512,1024]{1,0:T(8,128)(2,1)}, u32[]{:S(2)}) %copy-start) | copy-done | bytes 1048600
  20.3 0.0 copy-start.1
  20.3 1.4 %copy-done.1 = bf16[3,512,512]{2,1,0:T(8,128)(2,1)S(1)} copy-done((bf16[3,512,512]{2,1,0:T(8,128)(2,1)S(1)}, bf16[3,512,512]{2,1,0:T(8,128)(2,1)}, u32[]{:S(2)}) %copy-start.1) | copy-done | bytes 1572888
  21.7 0.0 copy-start.3
  21.7 1.0 %copy-done.3 = bf16[512,512]{1,0:T(8,128)(2,1)S(1)} copy-done((bf16[512,512]{1,0:T(8,128)(2,1)S(1)}, bf16[512,512]{1,0:T(8,128)(2,1)}, u32[]{:S(2)}) %copy-start.3) | copy-done | bytes 524312
  22.8 0.0 copy-start.4
  22.8 1.0 %copy-done.4 = bf16[512,512]{1,0:T(8,128)(2,1)S(1)} copy-done((bf16[512,512]{1,0:T(8,128)(2,1)S(1)}, bf16[512,512]{1,0:T(8,128)(2,1)}, u32[]{:S(2)}) %copy-start.4) | copy-done | bytes 524312
  23.8 0.0 copy-start.5
  23.8 0.9 %copy-done.5 = bf16[2,256,256]{2,1,0:T(8,128)(2,1)S(1)} copy-done((bf16[2,256,256]{2,1,0:T(8,128)(2,1)S(1)}, bf16[2,256,256]{2,1,0:T(8,128)(2,1)}, u32[]{:S(2)}) %copy-start.5) | copy-done | bytes 262168
  24.8 0.0 copy-start.6
  24.8 0.9 %copy-done.6 = f32[2,128,128]{2,1,0:T(8,128)S(1)} copy-done((f32[2,128,128]{2,1,0:T(8,128)S(1)}, f32[2,128,128]{2,1,0:T(8,128)}, u32[]{:S(2)}) %copy-start.6) | copy-done | bytes 131096
  25.7 0.0 copy-start.7
  25.7 0.7 %copy-done.7 = s32[4,8,128]{2,1,0:T(8,128)S(1)} copy-done((s32[4,8,128]{2,1,0:T(8,128)S(1)}, s32[4,8,128]{2,1,0:T(8,128)}, u32[]{:S(2)}) %copy-start.7) | copy-done | bytes 16408
  26.4 10.1 %tiles.1.part = bf16[256,256]{1,0:T(8,128)(2,1)S(1)} custom-call(bf16[512,2048]{1,0:T(8,128)(2,1)} %bitcast.12, bf16[512,1024]{1,0:T(8,128)(2,1)S(1)} %copy-done, bf16[512,512]{1,0:T(8,128)(2,1)S(1)} %copy-done.3, bf16[512,512]{1,0:T(8,128)(2,1)S(1)} %copy-done.4, s32[4,8,128]{2,1,0:T(8,128)S(1)} %copy-done.7, bf16[2,256,256]{2,1,0:T(8,128)(2,1)S(1)} %copy-done.5, ...), custom_call_target="tpu_custom_call" | custom-call | tf_op jit(solution)/shard_map/tiles/pallas_call | solution.py:369
  36.5 0.0 copy-start.2
  36.5 0.6 %copy-done.2 = bf16[256,256]{1,0:T(8,128)(2,1)} copy-done((bf16[256,256]{1,0:T(8,128)(2,1)}, bf16[256,256]{1,0:T(8,128)(2,1)S(1)}, u32[]{:S(2)}) %copy-start.2) | copy-done | bytes 131096
  37.1 0.6 %sub.10.keys = s32[1,256]{1,0:T(1,128)} reshape(s32[4,64]{1,0:T(4,128)S(1)} %subtract_reduce_fusion) | data formatting | bytes 2048 | tf_op jit(solution)/shard_map/sub | solution.py:410
  37.8 13.1 %residual.1 = (f32[128,128]{1,0:T(8,128)}, bf16[4,64,256]{2,1,0:T(8,128)(2,1)}) custom-call(bf16[256,256]{1,0:T(8,128)(2,1)} %copy-done.2, bf16[64,128,128]{2,1,0:T(8,128)(2,1)} %bitcast.11, f32[128,128]{1,0:T(8,128)} %bitcast.14, s32[1,64]{1,0:T(1,128)} %counts.1), custom_call_target="tpu_custom_call" | custom-call | tf_op jit(solution)/shard_map/residual/pallas_call | solution.py:388
  50.8 0.0 copy-start.8
  50.9 5.2 %dirty.1 = f32[8192,128]{1,0:T(8,128)} custom-call(s32[1,256]{1,0:T(1,128)} %sub.10.keys, bf16[256,256]{1,0:T(8,128)(2,1)} %bitcast.13), custom_call_target="tpu_custom_call" | custom-call | tf_op jit(solution)/shard_map/dirty/pallas_call | solution.py:412
  56.0 0.0 copy-done.8
  56.0 0.6 %copy.14 = f32[1,64,2,128]{3,2,1,0:T(2,128)} copy(f32[1,64,2,128]{3,2,1,0:T(2,128)S(1)} %bitcast.15) | data formatting | bytes 131072
  (2 shorter events, 0.0 us)
Async XLA Ops:
  19.1 1.2 %copy-start = (bf16[512,1024]{1,0:T(8,128)(2,1)S(1)}, bf16[512,1024]{1,0:T(8,128)(2,1)}, u32[]{:S(2)}) copy-start(bf16[512,1024]{1,0:T(8,128)(2,1)} %sky.3) | copy-start | bytes 3145732
  20.3 1.4 %copy-start.1 = (bf16[3,512,512]{2,1,0:T(8,128)(2,1)S(1)}, bf16[3,512,512]{2,1,0:T(8,128)(2,1)}, u32[]{:S(2)}) copy-start(bf16[3,512,512]{2,1,0:T(8,128)(2,1)} %constant.22.clone.pair_table) | copy-start | bytes 4718596
  21.7 1.0 %copy-start.3 = (bf16[512,512]{1,0:T(8,128)(2,1)S(1)}, bf16[512,512]{1,0:T(8,128)(2,1)}, u32[]{:S(2)}) copy-start(bf16[512,512]{1,0:T(8,128)(2,1)} %get-tuple-element.7.low) | copy-start | bytes 1572868
  22.8 1.0 %copy-start.4 = (bf16[512,512]{1,0:T(8,128)(2,1)S(1)}, bf16[512,512]{1,0:T(8,128)(2,1)}, u32[]{:S(2)}) copy-start(bf16[512,512]{1,0:T(8,128)(2,1)} %get-tuple-element.8.high) | copy-start | bytes 1572868
  23.8 0.9 %copy-start.5 = (bf16[2,256,256]{2,1,0:T(8,128)(2,1)S(1)}, bf16[2,256,256]{2,1,0:T(8,128)(2,1)}, u32[]{:S(2)}) copy-start(bf16[2,256,256]{2,1,0:T(8,128)(2,1)} %constant.21.clone.real_table) | copy-start | bytes 786436
  24.8 0.9 %copy-start.6 = (f32[2,128,128]{2,1,0:T(8,128)S(1)}, f32[2,128,128]{2,1,0:T(8,128)}, u32[]{:S(2)}) copy-start(f32[2,128,128]{2,1,0:T(8,128)} %constant.23.clone.phase) | copy-start | bytes 393220
  25.7 0.7 %copy-start.7 = (s32[4,8,128]{2,1,0:T(8,128)S(1)}, s32[4,8,128]{2,1,0:T(8,128)}, u32[]{:S(2)}) copy-start(s32[4,8,128]{2,1,0:T(8,128)} %get-tuple-element.9.codes) | copy-start | bytes 49156
  36.5 0.7 %copy-start.2 = (bf16[256,256]{1,0:T(8,128)(2,1)}, bf16[256,256]{1,0:T(8,128)(2,1)S(1)}, u32[]{:S(2)}) copy-start(bf16[256,256]{1,0:T(8,128)(2,1)S(1)} %tiles.1.part) | copy-start | bytes 393220
  50.8 5.2 %copy-start.8 = (f32[128,128]{1,0:T(8,128)S(1)}, f32[128,128]{1,0:T(8,128)}, u32[]{:S(2)}) copy-start(f32[128,128]{1,0:T(8,128)} %get-tuple-element.10) | copy-start | bytes 196612

commit v2 on v1

v2 whole, which is shorter than its diff:
```python
import functools
import math

import jax
import jax.numpy as jnp
import numpy as np
from jax import lax
from jax.experimental import pallas as pl
from jax.experimental.pallas import tpu as pltpu
from jax.sharding import PartitionSpec as P

MESH = pl.DeviceIdType.MESH
RADIX = 8
WIDE = 16
VMEM = pl.BlockSpec(memory_space=pltpu.VMEM)
HBM = pl.BlockSpec(memory_space=pltpu.HBM)
NT = (((1,), (1,)), ((), ()))
NN = (((1,), (0,)), ((), ()))


def wave(rows, cols, period, factor):
    angle = (np.outer(rows, cols) % period) * (2.0 * math.pi / period)
    return np.cos(angle) * factor, np.sin(angle) * factor


def first_tables(grid):
    span = grid // RADIX
    blocks = grid // 2 // RADIX
    cols = np.arange(span)

    def of(i):
        return wave(RADIX * np.arange(blocks) + i, cols, grid, grid**-0.5)

    real = []
    for i in (0, RADIX // 2):
        cos, sin = of(i)
        real.append(np.concatenate([cos, -sin], 0))
    pairs = []
    for i in range(1, RADIX // 2):
        cos, sin = of(i)
        cos_m, sin_m = of(RADIX - i)
        pairs.append(
            np.concatenate(
                [
                    np.concatenate([cos, sin], 1),
                    np.concatenate([-sin, cos], 1),
                    np.concatenate([cos_m, -sin_m], 1),
                    np.concatenate([-sin_m, -cos_m], 1),
                ],
                0,
            )
        )
    return np.stack(real).astype(jnp.bfloat16), np.stack(pairs).astype(jnp.bfloat16)


def second_tables(grid):
    period = grid // WIDE
    phase = np.stack(wave(np.arange(period), np.arange(period), period, 1.0), 1).astype(np.float32)
    cos, sin = wave(np.arange(grid), np.arange(WIDE), grid, grid**-0.5)
    cos, sin = np.tile(cos, (1, RADIX)), np.tile(sin, (1, RADIX))
    cos, sin = cos.reshape(-1, period, cos.shape[1]), sin.reshape(-1, period, sin.shape[1])
    table = np.concatenate([np.concatenate([cos, -sin], 2), np.concatenate([sin, cos], 2)], 1)
    return phase, table.astype(jnp.bfloat16)


def group_index():
    return lax.axis_index("bl") * lax.axis_size("pol") + lax.axis_index("pol")


def group_device(index):
    pol = lax.axis_size("pol")
    return {"bl": lax.div(index, pol), "pol": lax.rem(index, pol)}


def transform_rows(beams, at, pattern, strip, low, high, real_table, pair_table, g_real, g_pair, re, im):
    span = pattern.shape[1] // RADIX
    width = low.shape[1]
    beam = lax.axis_index("beam")
    step = 32
    root = math.sqrt(0.5)

    def fold(index, carry):
        src = pl.ds(pl.multiple_of(at + index * step, step), step)
        dst = pl.ds(pl.multiple_of(index * step, step), step)
        left = jnp.where(beam > 0, low[src, :], jnp.zeros((step, width), low.dtype))
        right = jnp.where(beam < beams - 1, high[src, :], jnp.zeros((step, width), high.dtype))
        window = jnp.concatenate([left, strip[src, :], right], axis=1)
        parts = []
        for a in range(RADIX):
            cut = slice(a * span, (a + 1) * span)
            weighted = pattern[src, cut].astype(jnp.float32) * window[:, cut].astype(jnp.float32)
            parts.append(weighted.astype(jnp.bfloat16).astype(jnp.float32))
        s = [parts[a] + parts[a + 4] for a in range(4)]
        d = [parts[a] - parts[a + 4] for a in range(4)]
        even, odd = s[0] + s[2], s[1] + s[3]
        near, far = root * (d[1] - d[3]), root * (d[1] + d[3])

        def put(ref, lead, off, value):
            ref[lead, dst, off : off + span] = value.astype(jnp.bfloat16)

        put(g_real, 0, 0, even + odd)
        put(g_real, 1, 0, even - odd)
        put(g_pair, 0, 0, d[0] + near)
        put(g_pair, 0, span, -(d[2] + far))
        put(g_pair, 1, 0, s[0] - s[2])
        put(g_pair, 1, span, s[3] - s[1])
        put(g_pair, 2, 0, d[0] - near)
        put(g_pair, 2, span, d[2] - far)
        return carry

    lax.fori_loop(0, g_real.shape[1] // step, fold, 0)
    blocks = re.shape[0]
    re = re.reshape(blocks * RADIX, re.shape[2])
    im = im.reshape(blocks * RADIX, im.shape[2])
    for k, i in enumerate((0, RADIX // 2)):
        out = lax.dot_general(real_table[k], g_real[k], NT, preferred_element_type=jnp.float32)
        re[pl.ds(i, blocks, stride=RADIX), :] = out[:blocks]
        im[pl.ds(i, blocks, stride=RADIX), :] = out[blocks:]
    for k in range(RADIX // 2 - 1):
        out = lax.dot_general(pair_table[k], g_pair[k], NT, preferred_element_type=jnp.float32)
        for n, (ref, i) in enumerate(((re, k + 1), (im, k + 1), (re, RADIX - 1 - k), (im, RADIX - 1 - k))):
            ref[pl.ds(i, blocks, stride=RADIX), :] = out[n * blocks : (n + 1) * blocks]


def asked_tiles(asker, codes, phase, weights, re, im, turned):
    period = phase.shape[2]
    vis = turned.shape[0] // RADIX
    cells = RADIX * WIDE
    own = lax.broadcasted_iota(jnp.int32, (RADIX, 2 * cells), 0)
    column = lax.broadcasted_iota(jnp.int32, (RADIX, 2 * cells), 1)
    keep = own == (column % cells) // WIDE

    def one(r):
        tile = codes[asker, 0, r]
        turn = phase[lax.rem(tile, period)]
        cos, sin = turn[0:1], turn[1:2]
        up = lax.div(tile, period)
        x, y = re[up], im[up]
        return jnp.concatenate([x * cos + y * sin, y * cos - x * sin], axis=1)

    def turn_pair(p, carry):
        both = jnp.concatenate([one(2 * p), one(2 * p + 1)], axis=0)
        turned[pl.ds(pl.multiple_of(p * 2 * RADIX, 2 * RADIX), 2 * RADIX), :] = both.astype(jnp.bfloat16)
        return carry

    lax.fori_loop(0, vis // 2, turn_pair, 0, unroll=8)
    cells_of = lax.dot_general(turned[...], weights, NN, preferred_element_type=jnp.float32)
    picked = jnp.where(keep[None], cells_of.reshape(vis, RADIX, 2 * cells), 0.0)
    return jnp.sum(picked, axis=1)


def predict_kernel(
    group, beams, tiles_dev,
    sky, pattern_in, kernels_in, observed, owner, place, counts, real_in, pair_in, phase_in, table_in,
    residual, shared, codes,
    strip, low, high, pattern, kernels, real_table, pair_table, phase, table, code, codes_s,
    g_real, g_pair, re, im, turned, total, part, came, given, wide, narrow,
    local, halo_send, halo_recv, code_send, code_recv, part_send, part_recv, share_send, share_recv,
):
    beam = lax.axis_index("beam")
    me = group_index()
    vis, cells = kernels.shape[0], kernels.shape[1]
    width = low.shape[1]
    period = phase.shape[2]
    chunks = pattern.shape[0] // period

    loads = []
    for n, (src, dst) in enumerate((
        (pattern_in, pattern), (sky, strip), (real_in, real_table), (pair_in, pair_table), (phase_in, phase),
        (table_in.at[pl.ds(me * chunks, chunks)], table), (kernels_in, kernels),
    )):
        load = pltpu.make_async_copy(src, dst, local.at[n])
        load.start()
        loads.append(load)

    named = jnp.broadcast_to(owner[...] * tiles_dev + place[...], (code.shape[0], vis))
    for n in range(code.shape[1] // vis):
        code[:, n * vis : (n + 1) * vis] = named

    barrier = pltpu.get_barrier_semaphore()
    has_next, has_last = beam < beams - 1, beam > 0

    def greet(device):
        pl.semaphore_signal(barrier, inc=1, device_id=device, device_id_type=MESH)

    for step in range(1, group):
        greet(group_device(lax.rem(me + step, group)))

    @pl.when(has_next)
    def _():
        greet({"beam": beam + 1})

    @pl.when(has_last)
    def _():
        greet({"beam": beam - 1})

    edges = jnp.where(beam < beams - 1, 1, 0) + jnp.where(beam > 0, 1, 0)
    pl.semaphore_wait(barrier, group - 1 + edges)

    def halo(side, k):
        rows = pl.ds(pl.multiple_of(k * period, period), period)
        first = 0 if side else sky.shape[1] - width
        return pltpu.make_async_remote_copy(
            src_ref=sky.at[rows, pl.ds(first, width)], dst_ref=(high if side else low).at[rows, :],
            send_sem=halo_send.at[side, k], recv_sem=halo_recv.at[side, k],
            device_id={"beam": beam - 1 if side else beam + 1}, device_id_type=MESH,
        )

    def to_peer(step, source, target, send, recv):
        return pltpu.make_async_remote_copy(
            src_ref=source, dst_ref=target,
            send_sem=send.at[step - 1], recv_sem=recv.at[step - 1],
            device_id=group_device(lax.rem(me + step, group)), device_id_type=MESH,
        )

    @pl.when(has_next)
    def _():
        for k in range(chunks):
            halo(0, k).start()

    @pl.when(has_last)
    def _():
        for k in range(chunks):
            halo(1, k).start()

    named_copies = [to_peer(step, code, codes.at[me], code_send, code_recv) for step in range(1, group)]
    for copy in named_copies:
        copy.start()
    codes[me] = code[...]
    total[...] = jnp.zeros_like(total)
    wide[...] = jnp.zeros_like(wide)
    for copy in named_copies:
        copy.wait()
    to_scalar = pltpu.make_async_copy(codes, codes_s, local.at[len(loads)])
    to_scalar.start()
    to_scalar.wait()
    for load in loads[:-1]:
        load.wait()

    def of_chunk(k, carry):
        @pl.when(has_last)
        def _():
            halo(0, k).wait_recv()

        @pl.when(has_next)
        def _():
            halo(1, k).wait_recv()

        transform_rows(
            beams, k * period, pattern, strip, low, high, real_table, pair_table, g_real, g_pair, re, im
        )

        def of_asker(step, inner):
            asker = lax.rem(me + step, group)
            rows = pl.ds(pl.multiple_of(asker * vis, vis), vis)
            total[rows, :] += asked_tiles(asker, codes_s, phase, table[k], re, im, turned)

            @pl.when((k == chunks - 1) & (step < group))
            def _():
                part[rows, :] = total[rows, :].astype(part.dtype)
                to_peer(step, part.at[rows, :], came.at[me], part_send, part_recv).start()

            return inner

        lax.fori_loop(1, group + 1, of_asker, 0)
        return carry

    lax.fori_loop(0, chunks, of_chunk, 0)

    own = lax.broadcasted_iota(jnp.int32, (vis, vis), 0) == lax.broadcasted_iota(jnp.int32, (vis, vis), 1)
    count = jnp.sum(jnp.where(own, counts[...].astype(jnp.float32), 0.0), axis=1, keepdims=True)
    mask = lax.broadcasted_iota(jnp.int32, (vis, cells), 1).astype(jnp.float32) < count
    mine = total[pl.ds(pl.multiple_of(me * vis, vis), vis), :]
    loads[-1].wait()
    for step in range(1, group):
        rows = pl.ds(pl.multiple_of(lax.rem(me + step, group) * vis, vis), vis)
        to_peer(step, part.at[rows, :], came.at[me], part_send, part_recv).wait()
    for step in range(1, group):
        mine = mine + came[lax.rem(me + step, group)].astype(jnp.float32)
    for c in range(2):
        wide[pl.ds(c, vis, stride=RADIX), :] = mine[:, c * cells : (c + 1) * cells]

    def apply(dims):
        def of_tile(r, carry):
            at = pl.ds(pl.multiple_of(r * RADIX, RADIX), RADIX)
            narrow[at, :] = lax.dot_general(
                wide[at, :].astype(jnp.bfloat16), kernels[r], dims, preferred_element_type=jnp.float32
            )
            return carry

        lax.fori_loop(0, vis, of_tile, 0, unroll=16)

    apply(NT)
    for c in range(2):
        seen = observed[pl.ds(c, vis, stride=2), :]
        left = jnp.where(mask, seen - narrow[pl.ds(c, vis, stride=RADIX), :], 0.0)
        residual[pl.ds(c, vis, stride=2), :] = left
        wide[pl.ds(c, vis, stride=RADIX), :] = left
    apply(NN)
    for c in range(2):
        given[:, c * cells : (c + 1) * cells] = narrow[pl.ds(c, vis, stride=RADIX), :].astype(given.dtype)
    given_copies = [to_peer(step, given, shared.at[me], share_send, share_recv) for step in range(1, group)]
    for copy in given_copies:
        copy.start()
    shared[me] = given[...]
    for copy in given_copies:
        copy.wait()

    @pl.when(has_next)
    def _():
        for k in range(chunks):
            halo(0, k).wait_send()

    @pl.when(has_last)
    def _():
        for k in range(chunks):
            halo(1, k).wait_send()


def dirty_kernel(vis, codes, terms, dirty):
    rows = dirty.shape[0] // 2
    cells = dirty.shape[1]
    group, _, lanes = codes.shape
    start = pl.program_id(0) * rows + group_index() * rows * pl.num_programs(0)
    each = lanes // vis
    lane = lax.broadcasted_iota(jnp.int32, (1, lanes), 1)
    keys = []
    for first in range(0, group, each):
        key = codes[first, 0:1, :]
        for n in range(1, each):
            key = jnp.where(lane < n * vis, key, codes[first + n, 0:1, :])
        keys.append(key)
    key = jnp.concatenate(keys, axis=1) - start
    tile = lax.broadcasted_iota(jnp.int32, (rows, key.shape[1]), 0)
    onehot = jnp.where(tile == key, 1.0, 0.0).astype(jnp.bfloat16)
    out = lax.dot_general(onehot, terms[...], NN, preferred_element_type=jnp.float32)
    for c in range(2):
        dirty[pl.ds(c, rows, stride=2), :] = out[:, c * cells : (c + 1) * cells]


def on_device(sky_model, beam_pattern, kernels, observed, tile_owner, tile_local, vis_count):
    group = lax.axis_size(("bl", "pol"))
    beams = lax.axis_size("beam")
    rows, grid = beam_pattern.shape[1:]
    strip = sky_model.shape[1]
    halo = (grid - strip) // 2
    vis, cells = kernels.shape[1], kernels.shape[3]
    tiles_dev = (grid // 2 // RADIX) * (grid // WIDE) // group
    lanes = 128
    f32, bf16 = jnp.float32, jnp.bfloat16
    real_table, pair_table = first_tables(grid)
    phase, table = second_tables(grid)
    span, period = grid // RADIX, grid // WIDE
    chunks = rows // period
    dma = pltpu.SemaphoreType.DMA

    residual, shared, codes = pl.pallas_call(
        functools.partial(predict_kernel, group, beams, tiles_dev),
        out_shape=(
            jax.ShapeDtypeStruct((vis * 2, cells), f32),
            jax.ShapeDtypeStruct((group, vis, 2 * cells), bf16),
            jax.ShapeDtypeStruct((group, 8, lanes), jnp.int32),
        ),
        in_specs=[HBM, HBM, HBM, VMEM, VMEM, VMEM, VMEM, HBM, HBM, HBM, HBM],
        out_specs=(VMEM, VMEM, VMEM),
        scratch_shapes=[
            pltpu.VMEM((rows, strip), bf16),
            pltpu.VMEM((rows, halo), bf16),
            pltpu.VMEM((rows, halo), bf16),
            pltpu.VMEM((rows, grid), bf16),
            pltpu.VMEM((vis, cells, cells), bf16),
            pltpu.VMEM(real_table.shape, bf16),
            pltpu.VMEM(pair_table.shape, bf16),
            pltpu.VMEM(phase.shape, f32),
            pltpu.VMEM((chunks, *table.shape[1:]), bf16),
            pltpu.VMEM((8, lanes), jnp.int32),
            pltpu.SMEM((group, 8, lanes), jnp.int32),
            pltpu.VMEM((2, period, span), bf16),
            pltpu.VMEM((RADIX // 2 - 1, period, 2 * span), bf16),
            pltpu.VMEM((grid // 2 // RADIX, RADIX, period), f32),
            pltpu.VMEM((grid // 2 // RADIX, RADIX, period), f32),
            pltpu.VMEM((vis * RADIX, 2 * period), bf16),
            pltpu.VMEM((group * vis, 2 * cells), f32),
            pltpu.VMEM((group * vis, 2 * cells), bf16),
            pltpu.VMEM((group, vis, 2 * cells), bf16),
            pltpu.VMEM((vis, 2 * cells), bf16),
            pltpu.VMEM((vis * RADIX, cells), f32),
            pltpu.VMEM((vis * RADIX, cells), f32),
            dma((8,)),
            dma((2, chunks)), dma((2, chunks)),
            dma((group - 1,)), dma((group - 1,)),
            dma((group - 1,)), dma((group - 1,)),
            dma((group - 1,)), dma((group - 1,)),
        ],
        compiler_params=pltpu.CompilerParams(
            collective_id=0, has_side_effects=True, vmem_limit_bytes=60 * 1024 * 1024
        ),
        name="predict",
    )(
        sky_model, beam_pattern[0], kernels[0], observed.reshape(vis * 2, cells),
        tile_owner.reshape(1, vis), tile_local, vis_count,
        jnp.asarray(real_table), jnp.asarray(pair_table), jnp.asarray(phase), jnp.asarray(table),
    )

    blocks = 8
    dirty = pl.pallas_call(
        functools.partial(dirty_kernel, vis),
        grid=(blocks,),
        out_shape=jax.ShapeDtypeStruct((tiles_dev * 2, cells), f32),
        in_specs=[
            pl.BlockSpec(codes.shape, lambda i: (0, 0, 0)),
            pl.BlockSpec((group * vis, 2 * cells), lambda i: (0, 0)),
        ],
        out_specs=pl.BlockSpec((tiles_dev * 2 // blocks, cells), lambda i: (i, 0)),
        name="dirty",
    )(codes, shared.reshape(group * vis, 2 * cells))
    return (
        residual.reshape(1, vis, 2, cells),
        dirty.reshape(1, tiles_dev, 2, cells),
    )


def solution(mesh):
    placed = (
        P(("tile", "bl", "pol"), "beam"),
        P(("tile", "beam"), ("bl", "pol"), None),
        P(("tile", "beam"), ("bl", "pol"), None, None),
        P(("tile", "beam"), ("bl", "pol"), None, None),
        P(("tile", "beam"), ("bl", "pol"), None),
        P(("tile", "beam"), ("bl", "pol")),
        P(("tile", "beam"), ("bl", "pol")),
    )
    return jax.shard_map(
        on_device,
        mesh=mesh,
        in_specs=placed,
        out_specs=(
            P(("tile", "beam"), ("bl", "pol"), None, None),
            P(("tile", "beam"), ("bl", "pol"), None, None),
        ),
        check_vma=False,
    )
```

time: 57.1 us -> 41.1 us (0.72)
  local copies, waits for them, and re-layouts: 9.81 us -> 0.63 us
  Pallas kernels: 45.4 us -> 39.6 us
  other arithmetic: 0.7 us -> 0 us
    unnamed x19 -> x3, local copies, waits for them, and re-layouts: 8.56 us -> 0.63 us
    pallas_call x4 -> x2, Pallas kernels: 45.4 us -> 39.6 us  [the longest x1 34.4 us: on_device(): pl.pallas_call(functools.partial(predict_kernel, group, beams, tiles_dev)...]
    add x1 -> x0, other arithmetic: 0.68 us -> none  [on_device(): code = tile_owner[0, :, 0] * tiles_dev + tile_local[0]]
    sub x1 -> x0, local copies, waits for them, and re-layouts: 0.64 us -> none  [on_device(): keys = codes[:, 0, :vis].reshape(1, group * vis) - group_index() * tiles_dev]
    broadcast_in_dim x1 -> x0, local copies, waits for them, and re-layouts: 0.6 us -> none  [on_device(): code = jnp.broadcast_to(jnp.pad(code, (0, lanes - vis))[None], (8, lanes))]
where the time goes in v2:
time: 41.1 us; the launch traced here: 40.9 us
  Pallas kernels  39.6 us (96%)
  between operations  0.65 us (2%)
  local copies, waits for them, and re-layouts  0.63 us (2%)
    pallas_call x1, Pallas kernels, on_device(): pl.pallas_call(functools.partial(predict_kernel, group, beams, tiles_dev)...  34.4 us
    pallas_call x1, Pallas kernels, on_device(): pl.pallas_call(functools.partial(dirty_kernel, vis), grid=(blocks,), out_...  5.28 us

profile of v2, /device:TPU:0, one launch (start us, length us, event | category | flops | bytes accessed | tf_op | source)
XLA Modules:
  0.0 40.9 jit_solution(5656713910541016687)
XLA Ops:
  0.6 34.4 %predict.1 = (f32[128,128]{1,0:T(8,128)}, bf16[4,64,256]{2,1,0:T(8,128)(2,1)}, s32[4,8,128]{2,1,0:T(8,128)}) custom-call(bf16[512,1024]{1,0:T(8,128)(2,1)} %sky.1, bf16[512,2048]{1,0:T(8,128)(2,1)} %bitcast.8, bf16[64,128,128]{2,1,0:T(8,128)(2,1)} %bitcast.9, f32[128,128]{1,0:T(8,128)} %bitcast.11, s32[1,64]{1,0:T(1,128)} %bitcast.13, s32[1,64]{1,0:T(1,128)} %place.1, ...), custom_call_target="tpu_custom_call" | custom-call | tf_op jit(solution)/shard_map/predict/pallas_call | solution.py:357
  35.0 0.0 copy-start
  35.0 5.3 %dirty.1 = f32[8192,128]{1,0:T(8,128)} custom-call(s32[4,8,128]{2,1,0:T(8,128)} %get-tuple-element.6.codes, bf16[256,256]{1,0:T(8,128)(2,1)} %bitcast.10), custom_call_target="tpu_custom_call" | custom-call | tf_op jit(solution)/shard_map/dirty/pallas_call | solution.py:406
  40.3 0.0 copy-done
  40.3 0.6 %copy.14 = f32[1,64,2,128]{3,2,1,0:T(2,128)} copy(f32[1,64,2,128]{3,2,1,0:T(2,128)S(1)} %bitcast.12) | data formatting | bytes 131072
Async XLA Ops:
  35.0 5.3 %copy-start = (f32[128,128]{1,0:T(8,128)S(1)}, f32[128,128]{1,0:T(8,128)}, u32[]{:S(2)}) copy-start(f32[128,128]{1,0:T(8,128)} %get-tuple-element.5) | copy-start | bytes 196612

commit v3 on v2

--- a/solution.py
+++ b/solution.py
@@ -132,9 +132,9 @@
 
     def one(r):
         tile = codes[asker, 0, r]
-        turn = phase[lax.rem(tile, period)]
+        turn = phase[jnp.bitwise_and(tile, period - 1)]
         cos, sin = turn[0:1], turn[1:2]
-        up = lax.div(tile, period)
+        up = lax.shift_right_logical(tile, period.bit_length() - 1)
         x, y = re[up], im[up]
         return jnp.concatenate([x * cos + y * sin, y * cos - x * sin], axis=1)
 
@@ -317,11 +317,12 @@
             halo(1, k).wait_send()
 
 
-def dirty_kernel(vis, codes, terms, dirty):
-    rows = dirty.shape[0] // 2
-    cells = dirty.shape[1]
+def dirty_kernel(vis, codes, terms, left, dirty, residual, held, sems):
+    blocks, rows, cells = held.shape
+    rows = rows // 2
     group, _, lanes = codes.shape
-    start = pl.program_id(0) * rows + group_index() * rows * pl.num_programs(0)
+    start = group_index() * rows * blocks
+    residual[...] = left[...]
     each = lanes // vis
     lane = lax.broadcasted_iota(jnp.int32, (1, lanes), 1)
     keys = []
@@ -332,10 +333,19 @@
         keys.append(key)
     key = jnp.concatenate(keys, axis=1) - start
     tile = lax.broadcasted_iota(jnp.int32, (rows, key.shape[1]), 0)
-    onehot = jnp.where(tile == key, 1.0, 0.0).astype(jnp.bfloat16)
-    out = lax.dot_general(onehot, terms[...], NN, preferred_element_type=jnp.float32)
-    for c in range(2):
-        dirty[pl.ds(c, rows, stride=2), :] = out[:, c * cells : (c + 1) * cells]
+    copies = []
+    for block in range(blocks):
+        onehot = jnp.where(tile == key - block * rows, 1.0, 0.0).astype(jnp.bfloat16)
+        out = lax.dot_general(onehot, terms[...], NN, preferred_element_type=jnp.float32)
+        for c in range(2):
+            held[block, pl.ds(c, rows, stride=2), :] = out[:, c * cells : (c + 1) * cells]
+        copy = pltpu.make_async_copy(
+            held.at[block], dirty.at[pl.ds(block * rows * 2, rows * 2), :], sems.at[block]
+        )
+        copy.start()
+        copies.append(copy)
+    for copy in copies:
+        copy.wait()
 
 
 def on_device(sky_model, beam_pattern, kernels, observed, tile_owner, tile_local, vis_count):
@@ -403,17 +413,17 @@
     )
 
     blocks = 8
-    dirty = pl.pallas_call(
+    dirty, residual = pl.pallas_call(
         functools.partial(dirty_kernel, vis),
-        grid=(blocks,),
-        out_shape=jax.ShapeDtypeStruct((tiles_dev * 2, cells), f32),
-        in_specs=[
-            pl.BlockSpec(codes.shape, lambda i: (0, 0, 0)),
-            pl.BlockSpec((group * vis, 2 * cells), lambda i: (0, 0)),
-        ],
-        out_specs=pl.BlockSpec((tiles_dev * 2 // blocks, cells), lambda i: (i, 0)),
+        out_shape=(
+            jax.ShapeDtypeStruct((tiles_dev * 2, cells), f32),
+            jax.ShapeDtypeStruct((vis * 2, cells), f32),
+        ),
+        in_specs=[VMEM, VMEM, VMEM],
+        out_specs=(HBM, VMEM),
+        scratch_shapes=[pltpu.VMEM((blocks, tiles_dev * 2 // blocks, cells), f32), dma((blocks,))],
         name="dirty",
-    )(codes, shared.reshape(group * vis, 2 * cells))
+    )(codes, shared.reshape(group * vis, 2 * cells), residual)
     return (
         residual.reshape(1, vis, 2, cells),
         dirty.reshape(1, tiles_dev, 2, cells),

time: 41.1 us -> 37.2 us (0.905)
  Pallas kernels: 39.6 us -> 36.4 us
  local copies, waits for them, and re-layouts: 0.63 us -> 0 us
    pallas_call x1, Pallas kernels: 34.4 us -> 32.5 us  [on_device(): pl.pallas_call(functools.partial(predict_kernel, group, beams, tiles_dev)...]
    pallas_call x1, Pallas kernels: 5.28 us -> 3.92 us  [on_device(): pl.pallas_call(functools.partial(dirty_kernel, vis), out_shape=(jax.Shape...]
    unnamed x3 -> x0, local copies, waits for them, and re-layouts: 0.63 us -> none
where the time goes in v3:
time: 37.2 us; the launch traced here: 37.1 us
  Pallas kernels  36.4 us (98%)
  between operations  0.64 us (2%)
    pallas_call x1, Pallas kernels, on_device(): pl.pallas_call(functools.partial(predict_kernel, group, beams, tiles_dev)...  32.5 us
    pallas_call x1, Pallas kernels, on_device(): pl.pallas_call(functools.partial(dirty_kernel, vis), out_shape=(jax.Shape...  3.92 us

profile of v3, /device:TPU:0, one launch (start us, length us, event | category | flops | bytes accessed | tf_op | source)
XLA Modules:
  0.0 37.1 jit_solution(9693363317926575507)
XLA Ops:
  0.6 32.5 %predict.1 = (f32[128,128]{1,0:T(8,128)}, bf16[4,64,256]{2,1,0:T(8,128)(2,1)}, s32[4,8,128]{2,1,0:T(8,128)}) custom-call(bf16[512,1024]{1,0:T(8,128)(2,1)} %sky.1, bf16[512,2048]{1,0:T(8,128)(2,1)} %bitcast.7, bf16[64,128,128]{2,1,0:T(8,128)(2,1)} %bitcast.8, f32[128,128]{1,0:T(8,128)} %bitcast.10, s32[1,64]{1,0:T(1,128)} %bitcast.11, s32[1,64]{1,0:T(1,128)} %place.1, ...), custom_call_target="tpu_custom_call" | custom-call | tf_op jit(solution)/shard_map/predict/pallas_call | solution.py:367
  33.1 3.9 %dirty.1 = (f32[8192,128]{1,0:T(8,128)}, f32[128,128]{1,0:T(8,128)}) custom-call(s32[4,8,128]{2,1,0:T(8,128)} %get-tuple-element.7.codes, bf16[256,256]{1,0:T(8,128)(2,1)} %bitcast.9, f32[128,128]{1,0:T(8,128)} %get-tuple-element.9.left), custom_call_target="tpu_custom_call" | custom-call | tf_op jit(solution)/shard_map/dirty/pallas_call | solution.py:416
